TPU v7x, 128 devices: a whole 4x4x4 slice. The times are simulated.
128 devices in a mesh: section: 4 (over y), wide: 8 (over z, x_hi), narrow: 4 (over x_lo, core).
Axes of the slice: x: 4 (x_hi: 2, x_lo: 2; x = x_hi * 2 + x_lo), y: 4, z: 4, core: 2. Of those that a mesh axis runs over, the one named last changes fastest.
Arguments:
- normed_inputs: bfloat16 [4, 4, 4, 768, 4096], P('section', 'narrow', None, 'wide'), may hold values from -160 to 160
- value_cotangent: bfloat16 [4, 4, 4, 768, 1024], P('section', 'narrow', None, 'wide'), may hold values from -6 to 6
- expert_hidden: bfloat16 [4, 4, 4, 256, 7168], P('section', 'narrow', None, None, 'wide'), may hold values from -40 to 40
- expert_cotangent: bfloat16 [4, 4, 4, 256, 4096], P('section', 'narrow', None, 'wide'), may hold values from -110 to 110
- slot_gate: bfloat16 [4, 4, 4, 256], P('section', 'narrow', None, 'wide'), may hold values from 0.25 to 1
- slot_count: int32 [4, 4, 4], P('section', 'narrow'), may hold values from 129 to 256, as said below
- expert_weight: bfloat16 [4, 7168, 4096], P('section', 'wide', 'narrow'), may hold values from -0.0625 to 0.0625
- expert_moment: float32 [4, 7168, 4096], P('section', 'wide', 'narrow'), may hold values from -6 to 6
- value_weight: bfloat16 [4, 4096, 1024], P('section', ('wide', 'narrow')), may hold values from -0.09375 to 0.09375
- value_moment: float32 [4, 4096, 1024], P('section', ('wide', 'narrow')), may hold values from -6 to 6
Outputs:
- expert_weight_next: bfloat16 [4, 7168, 4096], P('section', 'wide', 'narrow')
- expert_moment_next: float32 [4, 7168, 4096], P('section', 'wide', 'narrow')
- value_weight_next: bfloat16 [4, 4096, 1024], P('section', ('wide', 'narrow'))
- value_moment_next: float32 [4, 4096, 1024], P('section', ('wide', 'narrow'))
Inputs may be any that keep to these rules, and one draw needn't show every extreme that they name: The live slots of a micro-batch are slots 0 to slot_count - 1; in every layer and replica some micro-batch fills all 256 slots.
All inputs are finite; a program needn't handle non-finite values.
Results may differ from a plain program's by a relative error of at most 0.014.
Values may be sent and summed in bfloat16 or wider, within the bound.
A program may use at most 128 MiB of HBM per device.

v0:
```python
import math
import jax
import jax.numpy as jnp
from jax import lax
from jax.sharding import Mesh
from jax.sharding import PartitionSpec as P

D = 4096
FF = 7168
KV = 1024
WIDE = ("wide_0", "wide_1")
NARROW = ("narrow_0", "narrow_1")
WIDE_NARROW = ("wide_0", "wide_1", "narrow_0", "narrow_1")
SECTION_WIDE_NARROW = ("section", "wide_0", "wide_1", "narrow_0", "narrow_1")
MOMENTUM_DECAY = 0.9
STEP_RATE = 0.01


def over_axes(shard, axes):
    for axis in axes:
        shard = lax.psum(shard, axis)
    return shard


def on_device(
    normed_inputs,
    value_cotangent,
    expert_hidden,
    expert_cotangent,
    slot_gate,
    slot_count,
    expert_weight,
    expert_moment,
    value_weight,
    value_moment,
):
    input_rows = normed_inputs[0, 0].reshape(-1, normed_inputs.shape[-1])
    value_cot_rows = value_cotangent[0, 0].reshape(-1, value_cotangent.shape[-1])
    hidden_local = expert_hidden[0, 0]
    cotangent = expert_cotangent[0, 0]
    gate_local = slot_gate[0, 0]
    live_count = slot_count[0, 0]
    cot_piece = lax.all_gather(cotangent, WIDE, axis=1, tiled=True)
    gate_piece = lax.all_gather(gate_local, WIDE, axis=1, tiled=True)
    length = cot_piece.shape[1]
    positions = jnp.arange(length, dtype=jnp.int32)
    live = positions[None, :] < live_count[:, None]
    coefficient = jnp.where(
        live, gate_piece.astype(jnp.float32), jnp.zeros(gate_piece.shape, jnp.float32)
    )
    scaled = (coefficient[:, :, None] * cot_piece.astype(jnp.float32)).astype(jnp.bfloat16)
    summed = lax.dot_general(
        hidden_local, scaled, (((0, 1), (0, 1)), ((), ())), preferred_element_type=jnp.float32
    )
    expert_grad = lax.psum_scatter(
        summed.astype(jnp.bfloat16), NARROW, scatter_dimension=1, tiled=True
    ).astype(jnp.float32)
    value_grad = lax.psum_scatter(
        lax.dot_general(
            input_rows, value_cot_rows, (((0,), (0,)), ((), ())), preferred_element_type=jnp.float32
        ).astype(jnp.bfloat16),
        WIDE_NARROW,
        scatter_dimension=0,
        tiled=True,
    ).astype(jnp.float32)
    squares = jnp.sum(expert_grad * expert_grad) + jnp.sum(value_grad * value_grad)
    overall = over_axes(squares, SECTION_WIDE_NARROW)
    entry_count = lax.axis_size("section") * (FF * D + D * KV)
    factor = jnp.minimum(1.0, math.sqrt(entry_count) / jnp.sqrt(overall + 1e-06))
    expert_next = MOMENTUM_DECAY * expert_moment[0] + factor * expert_grad
    value_next = MOMENTUM_DECAY * value_moment[0] + factor * value_grad
    expert_weight_next = (expert_weight[0].astype(jnp.float32) - STEP_RATE * expert_next).astype(
        jnp.bfloat16
    )
    value_weight_next = (value_weight[0].astype(jnp.float32) - STEP_RATE * value_next).astype(
        jnp.bfloat16
    )
    return (expert_weight_next[None], expert_next[None], value_weight_next[None], value_next[None])


def solution(mesh):
    finer = Mesh(
        mesh.devices.reshape(mesh.shape["section"], 4, 2, 2, 2),
        ("section", "wide_0", "wide_1", "narrow_0", "narrow_1"),
    )
    in_specs = (
        P("section", NARROW, None, WIDE, None),
        P("section", NARROW, None, WIDE, None),
        P("section", NARROW, None, None, WIDE),
        P("section", NARROW, None, WIDE, None),
        P("section", NARROW, None, WIDE),
        P("section", NARROW, None),
        P("section", WIDE, NARROW),
        P("section", WIDE, NARROW),
        P("section", WIDE_NARROW, None),
        P("section", WIDE_NARROW, None),
    )
    out_specs = (
        P("section", WIDE, NARROW),
        P("section", WIDE, NARROW),
        P("section", WIDE_NARROW, None),
        P("section", WIDE_NARROW, None),
    )
    return jax.shard_map(
        on_device, mesh=finer, in_specs=in_specs, out_specs=out_specs, check_vma=False
    )
```

profile of v0, /device:TPU:1, one launch (start us, length us, event | category | flops | bytes accessed | tf_op | source)
XLA Modules:
  0.0 304.2 jit_solution(16088000934408733016)
XLA Ops:
  8.0 0.0 copy-start
  8.0 0.0 all-gather.4.cloned.1.call-start
  8.1 0.7 all-gather.4.cloned.1.call-update
  8.7 0.0 reduce-scatter.5.cloned.1.call-start
  8.8 1.1 copy-done
  9.9 7.9 %bitcast_convert_fusion = bf16[4096,1024]{1,0:T(8,128)(2,1)} fusion(bf16[1,1,4,96,4096]{4,3,2,1,0:T(8,128)(2,1)S(1)} %copy-done, bf16[1,1,4,96,1024]{4,3,2,1,0:T(8,128)(2,1)} %param.11), kind=kOutput, calls=%fused_computation.2 | convolution fusion | flops 3225419776 | bytes 12320768 | tf_op jit(solution)/shard_map/dot_general | solution.py:59
  17.8 0.0 reduce-scatter.5.cloned.1.call-update
  17.8 0.0 reduce-scatter.3.cloned.1.call-start
  17.8 0.6 copy-done.2
  18.4 0.1 copy.21
  18.6 31.8 %all-gather = bf16[1,1,4,256]{2,1,0,3:T(2,128)(2,1)S(1)} all-gather(bf16[1,1,4,32]{2,1,0,3:T(2,128)(2,1)S(1)} %copy.21), channel_id=2, replica_groups=mesh['section'=4,'wide_0'=4,'wide_1'=2,'narrow_0'=2,'narrow_1'=2] {'wide..., dimensions={3}, use_global_device_ids=true | all-gather | bytes 2304 | tf_op jit(solution)/shard_map/all_gather | solution.py:44
  50.3 0.1 convert_element_type.58
  50.5 0.1 copy.22
  50.6 70.8 %all-gather.4.cloned.1.call-done = bf16[1,1,4,256,4096]{4,3,2,1,0:T(8,128)(2,1)} async-done(((bf16[1,1,4,32,4096]{4,3,2,1,0:T(8,128)(2,1)}), bf16[1,1,4,256,4096]{4,3,2,1,0:T(8,128)(2,1)}) %all-gather.4.cloned.1.call-update) | async-done | bytes 8388624 | tf_op jit(solution)/shard_map/all_gather | solution.py:43
  121.4 14.1 %fusion.5 = bf16[896,4096]{0,1:T(8,128)(2,1)} fusion(bf16[1,1,4,256,4096]{4,3,2,1,0:T(8,128)(2,1)} %all-gather.4.cloned.1.call-done, f32[4,256]{1,0:T(4,128)S(1)} %copy.22, bf16[1,1,4,256,896]{4,3,2,1,0:T(8,128)(2,1)} %param.12), kind=kOutput, calls=%fused_computation.7 | convolution fusion | flops 7532445696 | bytes 17567744 | tf_op jit(solution)/shard_map/dot_general | solution.py:52
  135.6 0.0 reduce-scatter.3.cloned.1.call-update
  135.6 17.6 %reduce-scatter.5.cloned.1.call-done = bf16[128,1024]{1,0:T(8,128)(2,1)} async-done(((bf16[4096,1024]{1,0:T(8,128)(2,1)}), bf16[128,1024]{1,0:T(8,128)(2,1)}) %reduce-scatter.5.cloned.1.call-update) | async-done | bytes 262160 | tf_op jit(solution)/shard_map/reduce_scatter | solution.py:58
  153.2 1.7 fusion.16
  154.9 72.7 %reduce-scatter.3.cloned.1.call-done = bf16[896,1024]{0,1:T(8,128)(2,1)} async-done(((bf16[896,4096]{0,1:T(8,128)(2,1)}), bf16[896,1024]{0,1:T(8,128)(2,1)}) %reduce-scatter.3.cloned.1.call-update) | async-done | bytes 1835024 | tf_op jit(solution)/shard_map/reduce_scatter | solution.py:55
  227.6 3.0 %fusion.8 = f32[]{:T(128)} fusion(bf16[896,1024]{0,1:T(8,128)(2,1)} %reduce-scatter.3.cloned.1.call-done), kind=kLoop, calls=%fused_computation.10 | loop fusion | flops 2752511 | bytes 1835012 | tf_op jit(solution)/shard_map/reduce_sum | solution.py:66
  231.9 9.0 %psum.35 = f32[]{:T(128)} all-reduce(f32[]{:T(128)S(6)} %add.26), channel_id=1, replica_groups=mesh['section'=4,'wide_0'=4,'wide_1'=2,'narrow_0'=2,'narrow_1'=2] {'sect..., use_global_device_ids=true, to_apply=%region_4.5 | all-reduce | flops 1 | bytes 8 | tf_op jit(solution)/shard_map/psum | solution.py:21
  240.9 9.3 %psum.36 = f32[]{:T(128)} all-reduce(f32[]{:T(128)} %psum.35), channel_id=1, replica_groups=mesh['section'=4,'wide_0'=4,'wide_1'=2,'narrow_0'=2,'narrow_1'=2] {'wide..., use_global_device_ids=true, to_apply=%region_5.6 | all-reduce | flops 1 | bytes 8 | tf_op jit(solution)/shard_map/psum | solution.py:21
  250.2 5.9 %psum.37 = f32[]{:T(128)} all-reduce(f32[]{:T(128)} %psum.36), channel_id=1, replica_groups=mesh['section'=4,'wide_0'=4,'wide_1'=2,'narrow_0'=2,'narrow_1'=2] {'wide..., use_global_device_ids=true, to_apply=%region_6.7 | all-reduce | flops 1 | bytes 8 | tf_op jit(solution)/shard_map/psum | solution.py:21
  256.0 5.0 %copy.20 = f32[1,896,1024]{1,2,0:T(8,128)} copy(f32[1,896,1024]{2,1,0:T(8,128)} %param.17) | data formatting | bytes 7340032 | tf_op args[7]
  261.1 4.4 %psum.38 = f32[]{:T(128)} all-reduce(f32[]{:T(128)} %psum.37), channel_id=1, replica_groups=mesh['section'=4,'wide_0'=4,'wide_1'=2,'narrow_0'=2,'narrow_1'=2] {'narr..., use_global_device_ids=true, to_apply=%region_7.8 | all-reduce | flops 1 | bytes 8 | tf_op jit(solution)/shard_map/psum | solution.py:21
  265.4 3.8 %copy.19 = bf16[1,896,1024]{1,2,0:T(8,128)(2,1)} copy(bf16[1,896,1024]{2,1,0:T(8,128)(2,1)} %param.16) | data formatting | bytes 3670016 | tf_op args[6]
  269.2 9.4 %psum.39 = f32[]{:T(128)} all-reduce(f32[]{:T(128)} %psum.38), channel_id=1, replica_groups=mesh['section'=4,'wide_0'=4,'wide_1'=2,'narrow_0'=2,'narrow_1'=2] {'narr..., use_global_device_ids=true, to_apply=%region_8.9 | all-reduce | flops 1 | bytes 8 | tf_op jit(solution)/shard_map/psum | solution.py:21
  279.3 6.5 %fusion.12 = (f32[1,896,1024]{1,2,0:T(8,128)}, bf16[1,896,1024]{1,2,0:T(8,128)(2,1)}) fusion(bf16[896,1024]{0,1:T(8,128)(2,1)} %reduce-scatter.3.cloned.1.call-done, f32[1,896,1024]{1,2,0:T(8,128)} %copy.20, f32[]{:T(128)S(6)} %min_shard_map.3, bf16[1,896,1024]{1,2,0:T(8,128)(2,1)} %copy.19), kind=kLoop, calls=%fused_computation.15 | loop fusion | flops 7340032 | bytes 12845060 | tf_op jit(solution)/shard_map/broadcast_in_dim | solution.py:78
  285.8 3.8 %copy.24 = bf16[1,896,1024]{2,1,0:T(8,128)(2,1)} copy(bf16[1,896,1024]{1,2,0:T(8,128)(2,1)} %get-tuple-element.13) | data formatting | bytes 3670016
  289.6 5.0 %copy.25 = f32[1,896,1024]{2,1,0:T(8,128)} copy(f32[1,896,1024]{1,2,0:T(8,128)} %get-tuple-element.12) | data formatting | bytes 7340032
  294.6 0.0 copy-done.1
  294.6 2.1 fusion.19
  (5 shorter events, 0.0 us)
Async XLA Ops:
  8.0 1.9 copy-start
  8.0 113.4 %all-gather.4.cloned.1.call-start = ((), (), s32[]{:S(2)}) async-start(), calls=%async_computation.4 | async-start | bytes 9437184 | tf_op jit(solution)/shard_map/all_gather | solution.py:43
  8.7 144.4 %reduce-scatter.5.cloned.1.call-start = ((), (), s32[]{:S(2)}) async-start(), calls=%async_computation.3 | async-start | bytes 8650752 | tf_op jit(solution)/shard_map/reduce_scatter | solution.py:58
  17.8 0.7 copy-start.2
  17.8 32.7 %copy-start.3 = (s32[1,1,4]{2,1,0:T(1,128)S(1)}, s32[1,1,4]{2,1,0:T(1,128)}, u32[]{:S(2)}) copy-start(s32[1,1,4]{2,1,0:T(1,128)} %param.15) | copy-start | bytes 52
  17.8 209.8 %reduce-scatter.3.cloned.1.call-start = ((), (), s32[]{:S(2)}) async-start(), calls=%async_computation.2 | async-start | bytes 9175040 | tf_op jit(solution)/shard_map/reduce_scatter | solution.py:55
  289.6 5.0 %copy-start.1 = (bf16[128,1024]{1,0:T(8,128)(2,1)S(1)}, bf16[128,1024]{1,0:T(8,128)(2,1)}, u32[]{:S(2)}) copy-start(bf16[128,1024]{1,0:T(8,128)(2,1)} %reduce-scatter.5.cloned.1.call-done) | copy-start | bytes 786436
Sparse Core Ops, SparseCore 0:
  11.1 110.2 all-gather.3
Sparse Core Ops, SparseCore 1:
  17.9 135.2 reduce-scatter.4
  155.4 72.1 reduce-scatter.2
where the time goes:
time: 305 us; the launch traced here: 304 us
  waiting for transfers between devices  162 us (53%)
  blocking collectives  69.7 us (23%)
  matrix products  22 us (7%)
  local copies, waits for them, and re-layouts  19.5 us (6%)
  between operations  17.5 us (6%)
  other arithmetic  13.5 us (4%)
    reduce_scatter x1, waiting for transfers between devices, on_device(): lax.psum_scatter(summed.astype(jnp.bfloat16), NARROW, scatter_dimension=1...  72.7 us
    all_gather x1, waiting for transfers between devices, on_device(): cot_piece = lax.all_gather(cotangent, WIDE, axis=1, tiled=True)  70.8 us
    psum x5, blocking collectives, over_axes(): shard = lax.psum(shard, axis)  37.9 us
    all_gather x1, blocking collectives, on_device(): gate_piece = lax.all_gather(gate_local, WIDE, axis=1, tiled=True)  31.8 us
    unnamed x13, local copies, waits for them, and re-layouts  19.4 us
    reduce_scatter x1, waiting for transfers between devices, on_device(): lax.psum_scatter(lax.dot_general(input_rows, value_cot_rows, (((0,), (0,)...  17.6 us
    dot_general x1, matrix products, on_device(): lax.dot_general(hidden_local, scaled, (((0, 1), (0, 1)), ((), ())), prefe...  14.1 us
    dot_general x1, matrix products, on_device(): lax.dot_general(input_rows, value_cot_rows, (((0,), (0,)), ((), ())), pre...  7.87 us
  transfers between devices with their start and end apart: 3, of which 3 were waited for; matrix products, arithmetic and copies ran while one was open for 8% of the time, Pallas kernels for 0%

commit v1 on v0

--- a/solution.py
+++ b/solution.py
@@ -41,7 +41,10 @@
     gate_local = slot_gate[0, 0]
     live_count = slot_count[0, 0]
     cot_piece = lax.all_gather(cotangent, WIDE, axis=1, tiled=True)
-    gate_piece = lax.all_gather(gate_local, WIDE, axis=1, tiled=True)
+    peers = lax.axis_size(WIDE)
+    shards = jnp.stack([gate_local for _ in range(peers)])
+    shards = lax.all_to_all(shards, WIDE, split_axis=0, concat_axis=0)
+    gate_piece = jnp.concatenate(shards, axis=1)
     length = cot_piece.shape[1]
     positions = jnp.arange(length, dtype=jnp.int32)
     live = positions[None, :] < live_count[:, None]

time: 305 us -> 304 us (level)
  blocking collectives: 69.7 us -> 52.6 us
  waiting for transfers between devices: 162 us -> 178 us
    all_gather x1 -> x0, blocking collectives: 31.8 us -> none  [on_device(): gate_piece = lax.all_gather(gate_local, WIDE, axis=1, tiled=True)]
    all_gather x1, waiting for transfers between devices: 70.8 us -> 86.8 us  [on_device(): cot_piece = lax.all_gather(cotangent, WIDE, axis=1, tiled=True)]
    all_to_all x0 -> x1, blocking collectives: none -> 14.7 us  [on_device(): shards = lax.all_to_all(shards, WIDE, split_axis=0, concat_axis=0)]
    unnamed x13 -> x12, local copies, waits for them, and re-layouts: 19.4 us -> 19.3 us
where the time goes in v1:
time: 304 us; the launch traced here: 303 us
  waiting for transfers between devices  178 us (59%)
  blocking collectives  52.6 us (17%)
  matrix products  22 us (7%)
  local copies, waits for them, and re-layouts  19.4 us (6%)
  between operations  17.5 us (6%)
  other arithmetic  13.4 us (4%)
    all_gather x1, waiting for transfers between devices, on_device(): cot_piece = lax.all_gather(cotangent, WIDE, axis=1, tiled=True)  86.8 us
    reduce_scatter x1, waiting for transfers between devices, on_device(): lax.psum_scatter(summed.astype(jnp.bfloat16), NARROW, scatter_dimension=1...  72.7 us
    psum x5, blocking collectives, over_axes(): shard = lax.psum(shard, axis)  37.9 us
    unnamed x12, local copies, waits for them, and re-layouts  19.3 us
    reduce_scatter x1, waiting for transfers between devices, on_device(): lax.psum_scatter(lax.dot_general(input_rows, value_cot_rows, (((0,), (0,)...  17.6 us
    all_to_all x1, blocking collectives, on_device(): shards = lax.all_to_all(shards, WIDE, split_axis=0, concat_axis=0)  14.7 us
    dot_general x1, matrix products, on_device(): lax.dot_general(hidden_local, scaled, (((0, 1), (0, 1)), ((), ())), prefe...  14.1 us
    dot_general x1, matrix products, on_device(): lax.dot_general(input_rows, value_cot_rows, (((0,), (0,)), ((), ())), pre...  7.87 us
  transfers between devices with their start and end apart: 3, of which 3 were waited for; matrix products, arithmetic and copies ran while one was open for 8% of the time, Pallas kernels for 0%

profile of v1, /device:TPU:1, one launch (start us, length us, event | category | flops | bytes accessed | tf_op | source)
XLA Modules:
  0.0 302.8 jit_solution(6363602383829753946)
XLA Ops:
  8.0 0.0 copy-start
  8.0 0.0 all-gather.3.cloned.1.call-start
  8.1 0.7 all-gather.3.cloned.1.call-update
  8.7 0.0 reduce-scatter.5.cloned.1.call-start
  8.8 1.1 copy-done
  9.9 7.9 %bitcast_convert_fusion = bf16[4096,1024]{1,0:T(8,128)(2,1)} fusion(bf16[1,1,4,96,4096]{4,3,2,1,0:T(8,128)(2,1)S(1)} %copy-done, bf16[1,1,4,96,1024]{4,3,2,1,0:T(8,128)(2,1)} %param.11), kind=kOutput, calls=%fused_computation.2 | convolution fusion | flops 3225419776 | bytes 12320768 | tf_op jit(solution)/shard_map/dot_general | solution.py:62
  17.8 0.0 reduce-scatter.5.cloned.1.call-update
  17.8 0.0 reduce-scatter.3.cloned.1.call-start
  17.8 0.6 copy-done.2
  18.4 14.7 %all_to_all.5 = bf16[8,4,32]{2,1,0:T(4,128)(2,1)S(1)} all-to-all(bf16[8,4,32]{2,1,0:T(4,128)(2,1)S(1)} %stack.3), channel_id=1, replica_groups=mesh['section'=4,'wide_0'=4,'wide_1'=2,'narrow_0'=2,'narrow_1'=2] {'wide..., dimensions={0} | all-to-all | bytes 4096 | tf_op jit(solution)/shard_map/all_to_all | solution.py:46
  33.2 0.1 reshape.61
  33.3 0.0 copy-done.3
  33.3 0.1 fusion.21
  33.4 86.8 %all-gather.3.cloned.1.call-done = bf16[1,1,4,256,4096]{4,3,2,1,0:T(8,128)(2,1)} async-done(((bf16[1,1,4,32,4096]{4,3,2,1,0:T(8,128)(2,1)}), bf16[1,1,4,256,4096]{4,3,2,1,0:T(8,128)(2,1)}) %all-gather.3.cloned.1.call-update) | async-done | bytes 8388624 | tf_op jit(solution)/shard_map/all_gather | solution.py:43
  120.1 14.1 %fusion.5 = bf16[896,4096]{0,1:T(8,128)(2,1)} fusion(bf16[1,1,4,256,4096]{4,3,2,1,0:T(8,128)(2,1)} %all-gather.3.cloned.1.call-done, f32[4,256]{1,0:T(4,128)S(1)} %fusion.21, bf16[1,1,4,256,896]{4,3,2,1,0:T(8,128)(2,1)} %param.12), kind=kOutput, calls=%fused_computation.7 | convolution fusion | flops 7532445696 | bytes 17567744 | tf_op jit(solution)/shard_map/dot_general | solution.py:55
  134.2 0.0 reduce-scatter.3.cloned.1.call-update
  134.3 17.6 %reduce-scatter.5.cloned.1.call-done = bf16[128,1024]{1,0:T(8,128)(2,1)} async-done(((bf16[4096,1024]{1,0:T(8,128)(2,1)}), bf16[128,1024]{1,0:T(8,128)(2,1)}) %reduce-scatter.5.cloned.1.call-update) | async-done | bytes 262160 | tf_op jit(solution)/shard_map/reduce_scatter | solution.py:61
  151.9 1.7 fusion.16
  153.5 72.7 %reduce-scatter.3.cloned.1.call-done = bf16[896,1024]{0,1:T(8,128)(2,1)} async-done(((bf16[896,4096]{0,1:T(8,128)(2,1)}), bf16[896,1024]{0,1:T(8,128)(2,1)}) %reduce-scatter.3.cloned.1.call-update) | async-done | bytes 1835024 | tf_op jit(solution)/shard_map/reduce_scatter | solution.py:58
  226.3 3.0 %fusion.8 = f32[]{:T(128)} fusion(bf16[896,1024]{0,1:T(8,128)(2,1)} %reduce-scatter.3.cloned.1.call-done), kind=kLoop, calls=%fused_computation.10 | loop fusion | flops 2752511 | bytes 1835012 | tf_op jit(solution)/shard_map/reduce_sum | solution.py:69
  230.6 9.0 %psum.35 = f32[]{:T(128)} all-reduce(f32[]{:T(128)S(6)} %add.26), channel_id=1, replica_groups=mesh['section'=4,'wide_0'=4,'wide_1'=2,'narrow_0'=2,'narrow_1'=2] {'sect..., use_global_device_ids=true, to_apply=%region_4.5 | all-reduce | flops 1 | bytes 8 | tf_op jit(solution)/shard_map/psum | solution.py:21
  239.6 9.3 %psum.36 = f32[]{:T(128)} all-reduce(f32[]{:T(128)} %psum.35), channel_id=1, replica_groups=mesh['section'=4,'wide_0'=4,'wide_1'=2,'narrow_0'=2,'narrow_1'=2] {'wide..., use_global_device_ids=true, to_apply=%region_5.6 | all-reduce | flops 1 | bytes 8 | tf_op jit(solution)/shard_map/psum | solution.py:21
  248.8 5.9 %psum.37 = f32[]{:T(128)} all-reduce(f32[]{:T(128)} %psum.36), channel_id=1, replica_groups=mesh['section'=4,'wide_0'=4,'wide_1'=2,'narrow_0'=2,'narrow_1'=2] {'wide..., use_global_device_ids=true, to_apply=%region_6.7 | all-reduce | flops 1 | bytes 8 | tf_op jit(solution)/shard_map/psum | solution.py:21
  254.7 5.0 %copy.25 = f32[1,896,1024]{1,2,0:T(8,128)} copy(f32[1,896,1024]{2,1,0:T(8,128)} %param.17) | data formatting | bytes 7340032 | tf_op args[7]
  259.7 4.4 %psum.38 = f32[]{:T(128)} all-reduce(f32[]{:T(128)} %psum.37), channel_id=1, replica_groups=mesh['section'=4,'wide_0'=4,'wide_1'=2,'narrow_0'=2,'narrow_1'=2] {'narr..., use_global_device_ids=true, to_apply=%region_7.8 | all-reduce | flops 1 | bytes 8 | tf_op jit(solution)/shard_map/psum | solution.py:21
  264.1 3.8 %copy.24 = bf16[1,896,1024]{1,2,0:T(8,128)(2,1)} copy(bf16[1,896,1024]{2,1,0:T(8,128)(2,1)} %param.16) | data formatting | bytes 3670016 | tf_op args[6]
  267.9 9.4 %psum.39 = f32[]{:T(128)} all-reduce(f32[]{:T(128)} %psum.38), channel_id=1, replica_groups=mesh['section'=4,'wide_0'=4,'wide_1'=2,'narrow_0'=2,'narrow_1'=2] {'narr..., use_global_device_ids=true, to_apply=%region_8.9 | all-reduce | flops 1 | bytes 8 | tf_op jit(solution)/shard_map/psum | solution.py:21
  278.0 6.5 %fusion.12 = (f32[1,896,1024]{1,2,0:T(8,128)}, bf16[1,896,1024]{1,2,0:T(8,128)(2,1)}) fusion(bf16[896,1024]{0,1:T(8,128)(2,1)} %reduce-scatter.3.cloned.1.call-done, f32[1,896,1024]{1,2,0:T(8,128)} %copy.25, f32[]{:T(128)S(6)} %min_shard_map.3, bf16[1,896,1024]{1,2,0:T(8,128)(2,1)} %copy.24), kind=kLoop, calls=%fused_computation.15 | loop fusion | flops 7340032 | bytes 12845060 | tf_op jit(solution)/shard_map/broadcast_in_dim | solution.py:81
  284.5 3.8 %copy.28 = bf16[1,896,1024]{2,1,0:T(8,128)(2,1)} copy(bf16[1,896,1024]{1,2,0:T(8,128)(2,1)} %get-tuple-element.17) | data formatting | bytes 3670016
  288.3 5.0 %copy.29 = f32[1,896,1024]{2,1,0:T(8,128)} copy(f32[1,896,1024]{1,2,0:T(8,128)} %get-tuple-element.16) | data formatting | bytes 7340032
  293.3 0.0 copy-done.1
  293.3 2.1 fusion.19
  (6 shorter events, 0.0 us)
Async XLA Ops:
  8.0 1.9 copy-start
  8.0 112.1 %all-gather.3.cloned.1.call-start = ((), (), s32[]{:S(2)}) async-start(), calls=%async_computation.5 | async-start | bytes 9437184 | tf_op jit(solution)/shard_map/all_gather | solution.py:43
  8.7 143.1 %reduce-scatter.5.cloned.1.call-start = ((), (), s32[]{:S(2)}) async-start(), calls=%async_computation.4 | async-start | bytes 8650752 | tf_op jit(solution)/shard_map/reduce_scatter | solution.py:61
  17.8 0.7 copy-start.2
  17.8 15.5 %copy-start.3 = (s32[1,1,4]{2,1,0:T(1,128)S(1)}, s32[1,1,4]{2,1,0:T(1,128)}, u32[]{:S(2)}) copy-start(s32[1,1,4]{2,1,0:T(1,128)} %param.15) | copy-start | bytes 52
  17.8 208.5 %reduce-scatter.3.cloned.1.call-start = ((), (), s32[]{:S(2)}) async-start(), calls=%async_computation.3 | async-start | bytes 9175040 | tf_op jit(solution)/shard_map/reduce_scatter | solution.py:58
  288.3 5.0 %copy-start.1 = (bf16[128,1024]{1,0:T(8,128)(2,1)S(1)}, bf16[128,1024]{1,0:T(8,128)(2,1)}, u32[]{:S(2)}) copy-start(bf16[128,1024]{1,0:T(8,128)(2,1)} %reduce-scatter.5.cloned.1.call-done) | copy-start | bytes 786436
Sparse Core Ops, SparseCore 0:
  11.1 108.9 all-gather.2
Sparse Core Ops, SparseCore 1:
  17.9 133.9 reduce-scatter.4
  154.1 72.1 reduce-scatter.2
